TPU v7x, 32 devices: a whole 2x2x4 slice. The times are simulated.
32 devices in a mesh: ctx: 16 (over z, y, core), head: 2 (over x).
Axes of the slice: x: 2, y: 2, z: 4, core: 2. Of those that a mesh axis runs over, the one named last changes fastest.
Arguments:
- queries: bfloat16 [16, 1024, 2048], P('ctx', None, 'head'), may hold values from -8 to 8
- keys: bfloat16 [16, 1024, 2048], P('ctx', None, 'head'), may hold values from -8 to 8
- values: bfloat16 [16, 1024, 2048], P('ctx', None, 'head'), may hold values from -24 to 24
- w_out: bfloat16 [2048, 4096], P('head'), may hold values from -0.125 to 0.125
Outputs:
- mixed: bfloat16 [16, 1024, 4096], P('ctx', 'head')
All inputs are finite; a program needn't handle non-finite values.
Results may differ from a plain program's by a relative error of at most 0.013.
Values may be sent and summed in bfloat16 or wider, within the bound.
A program may use at most 128 MiB of HBM per device.

v0:
```python
import jax
import jax.numpy as jnp
from jax import lax
from jax.sharding import PartitionSpec as P

HD = 128
GROUP = 4
masked_score = -1e30


def split_kinds(tensor, parity):
    groups = tensor.shape[2] // (2 * GROUP * HD)
    shaped = tensor.reshape((tensor.shape[0], tensor.shape[1], groups, 2, GROUP, HD))
    return shaped[:, :, :, parity].reshape((tensor.shape[0], tensor.shape[1], groups * GROUP, HD))


def normalized(scores):
    top = jnp.max(scores, axis=-1, keepdims=True)
    expo = jnp.exp(scores - top)
    total = jnp.sum(expo, axis=-1, keepdims=True)
    return (expo / total).astype(jnp.bfloat16)


def row_attention(queries, keys, values):
    scale = jnp.float32(1.0 / HD**0.5)
    length = queries.shape[1]
    causal = lax.broadcasted_iota(jnp.int32, (length, length), 1) <= lax.broadcasted_iota(
        jnp.int32, (length, length), 0
    )

    def one_row(triple):
        query_row, key_row, value_row = triple
        scores = (
            jnp.einsum("qhd,khd->hqk", query_row, key_row, preferred_element_type=jnp.float32)
            * scale
        )
        scores = jnp.where(causal, scores, masked_score)
        weights = normalized(scores)
        return jnp.einsum(
            "hqk,khd->qhd", weights, value_row, preferred_element_type=jnp.float32
        ).astype(jnp.bfloat16)

    return lax.map(one_row, (queries, keys, values))


def column_attention(triple):
    queries, keys, values = triple
    scale = jnp.float32(1.0 / HD**0.5)
    height = queries.shape[0]
    causal = lax.broadcasted_iota(jnp.int32, (height, height), 1) <= lax.broadcasted_iota(
        jnp.int32, (height, height), 0
    )
    scores = (
        jnp.einsum("rchd,schd->chrs", queries, keys, preferred_element_type=jnp.float32) * scale
    )
    scores = jnp.where(causal, scores, masked_score)
    weights = normalized(scores)
    attended = jnp.einsum(
        "chrs,schd->rchd", weights, values, preferred_element_type=jnp.float32
    ).astype(jnp.bfloat16)
    return lax.all_to_all(attended, "ctx", split_axis=0, concat_axis=1, tiled=True)


def on_device(queries, keys, values, w_out):
    rows_dev, stride, local_feat = queries.shape
    model_width = w_out.shape[1]
    groups = local_feat // (2 * GROUP * HD)
    row_out = row_attention(split_kinds(queries, 0), split_kinds(keys, 0), split_kinds(values, 0))
    col_triple = (split_kinds(queries, 1), split_kinds(keys, 1), split_kinds(values, 1))
    col_out = column_attention(
        (
            lax.all_to_all(col_triple[0], "ctx", split_axis=1, concat_axis=0, tiled=True),
            lax.all_to_all(col_triple[1], "ctx", split_axis=1, concat_axis=0, tiled=True),
            lax.all_to_all(col_triple[2], "ctx", split_axis=1, concat_axis=0, tiled=True),
        )
    )
    shaped = w_out.reshape((groups, 2, GROUP * HD, model_width))
    row_weights = shaped[:, 0].reshape((groups * GROUP * HD, model_width))
    col_weights = shaped[:, 1].reshape((groups * GROUP * HD, model_width))
    partial_value = jnp.dot(
        row_out.reshape((rows_dev * stride, -1)), row_weights, preferred_element_type=jnp.float32
    )
    partial_value = partial_value + jnp.dot(
        col_out.reshape((rows_dev * stride, -1)), col_weights, preferred_element_type=jnp.float32
    )
    partial_value = partial_value.reshape((rows_dev, stride, model_width))
    return lax.psum_scatter(
        partial_value.astype(jnp.bfloat16), "head", scatter_dimension=1, tiled=True
    )


def solution(mesh):
    return jax.shard_map(
        on_device,
        mesh=mesh,
        in_specs=(
            P("ctx", None, "head"),
            P("ctx", None, "head"),
            P("ctx", None, "head"),
            P("head", None),
        ),
        out_specs=P("ctx", "head", None),
        check_vma=False,
    )
```

profile of v0, /device:TPU:0, one launch (start us, length us, event | category | flops | bytes accessed | tf_op | source)
XLA Modules:
  0.0 254.6 jit_solution(13111694995554107261)
XLA Ops:
  6.5 2.9 %copy.35 = bf16[1,1024,1024]{1,2,0:T(8,128)(2,1)S(1)} copy(bf16[1,1024,1024]{2,1,0:T(8,128)(2,1)} %param.4) | data formatting | bytes 4194304 | tf_op args[0]
  9.4 0.0 copy-start
  9.4 0.1 slice_bitcast_fusion.6
  9.5 1.6 copy.41
  11.1 7.4 %all-to-all-start = ((bf16[1,1024,4,128]{3,2,0,1:T(4,128)(2,1)}), bf16[1,1024,4,128]{3,2,0,1:T(4,128)(2,1)S(1)}, u32[]{:S(2)}, u32[]{:S(2)}) async-start(bf16[1,1024,4,128]{3,2,0,1:T(4,128)(2,1)} %copy.41), calls=%async_computation | async-start | bytes 2097152 | tf_op jit(solution)/shard_map/all_to_all | solution.py:72
  18.5 4.0 %copy.37 = bf16[1,1024,1024]{1,2,0:T(8,128)(2,1)} copy(bf16[1,1024,1024]{2,1,0:T(8,128)(2,1)} %param.5) | data formatting | bytes 4194304 | tf_op args[1]
  22.5 0.0 copy-done
  22.5 1.3 slice_bitcast_fusion.5
  23.8 1.4 copy.43
  25.2 16.2 %all-to-all-done = bf16[1,1024,4,128]{3,2,0,1:T(4,128)(2,1)S(1)} async-done(((bf16[1,1024,4,128]{3,2,0,1:T(4,128)(2,1)}), bf16[1,1024,4,128]{3,2,0,1:T(4,128)(2,1)S(1)}, u32[]{:S(2)}, u32[]{:S(2)}) %all-to-all-start) | async-done | bytes 1048608 | tf_op jit(solution)/shard_map/all_to_all | solution.py:72
  41.4 6.8 %all-to-all-start.1 = ((bf16[1,1024,4,128]{3,2,0,1:T(4,128)(2,1)}), bf16[1,1024,4,128]{3,2,0,1:T(4,128)(2,1)}, u32[]{:S(2)}, u32[]{:S(2)}) async-start(bf16[1,1024,4,128]{3,2,0,1:T(4,128)(2,1)} %copy.43), calls=%async_computation.1 | async-start | bytes 2097152 | tf_op jit(solution)/shard_map/all_to_all | solution.py:73
  48.3 2.9 %copy.39 = bf16[1,1024,1024]{1,2,0:T(8,128)(2,1)S(1)} copy(bf16[1,1024,1024]{2,1,0:T(8,128)(2,1)} %param.6) | data formatting | bytes 4194304 | tf_op args[2]
  51.1 0.0 copy-done.1
  51.1 0.1 slice_bitcast_fusion.4
  51.2 1.5 copy.47
  52.7 18.5 %all-to-all-done.1 = bf16[1,1024,4,128]{3,2,0,1:T(4,128)(2,1)} async-done(((bf16[1,1024,4,128]{3,2,0,1:T(4,128)(2,1)}), bf16[1,1024,4,128]{3,2,0,1:T(4,128)(2,1)}, u32[]{:S(2)}, u32[]{:S(2)}) %all-to-all-start.1) | async-done | bytes 1048608 | tf_op jit(solution)/shard_map/all_to_all | solution.py:73
  71.2 6.8 %all-to-all-start.2 = ((bf16[1,1024,4,128]{3,2,0,1:T(4,128)(2,1)}), bf16[1,1024,4,128]{3,2,0,1:T(4,128)(2,1)}, u32[]{:S(2)}, u32[]{:S(2)}) async-start(bf16[1,1024,4,128]{3,2,0,1:T(4,128)(2,1)} %copy.47), calls=%async_computation.2 | async-start | bytes 2097152 | tf_op jit(solution)/shard_map/all_to_all | solution.py:74
  78.1 1.3 iota_compare_fusion
  79.4 11.8 %fusion.29 = (f32[4,1024]{1,0:T(4,128)S(1)}, f32[4,1024,1024]{1,2,0:T(8,128)}) fusion(pred[1024,1024]{0,1:T(8,128)(4,1)} %iota_compare_fusion, bf16[1,1024,1,2,4,128]{1,5,4,3,2,0:T(8,128)(2,1)} %bitcast.62, bf16[1,1024,1,2,4,128]{1,5,4,3,2,0:T(8,128)(2,1)} %bitcast.64), kind=kOutput, calls=%fused_computation.46 | convolution fusion | flops 1090520064 | bytes 19939328 | tf_op jit(solution)/shard_map/while/body/eval_jaxpr/sub | solution.py:19
  91.2 0.0 copy-done.2
  91.2 4.6 %fusion.30 = (f32[64,4,16]{2,1,0:T(4,128)S(1)}, f32[64,4,16,16]{2,3,1,0:T(8,128)}) fusion(pred[16,16]{0,1:T(8,128)(4,1)S(1)} %iota_compare_fusion.1, bf16[16,64,4,128]{3,2,1,0:T(4,128)(2,1)} %bitcast.13, bf16[16,64,4,128]{3,2,1,0:T(4,128)(2,1)S(1)} %bitcast.65), kind=kOutput, calls=%fused_computation.47 | convolution fusion | flops 17039376 | bytes 2375936 | tf_op jit(solution)/shard_map/sub | solution.py:19
  95.8 5.2 %all-to-all-done.2 = bf16[1,1024,4,128]{3,2,0,1:T(4,128)(2,1)} async-done(((bf16[1,1024,4,128]{3,2,0,1:T(4,128)(2,1)}), bf16[1,1024,4,128]{3,2,0,1:T(4,128)(2,1)}, u32[]{:S(2)}, u32[]{:S(2)}) %all-to-all-start.2) | async-done | bytes 1048608 | tf_op jit(solution)/shard_map/all_to_all | solution.py:74
  101.0 2.7 %fusion.13 = bf16[16,64,4,128]{3,0,2,1:T(8,128)(2,1)S(1)} fusion(f32[64,4,16,16]{2,3,1,0:T(8,128)} %get-tuple-element.24, bf16[16,64,4,128]{3,2,1,0:T(4,128)(2,1)} %bitcast.15, f32[64,4,16]{2,1,0:T(4,128)S(1)} %get-tuple-element.17), kind=kOutput, calls=%fused_computation.23 | convolution fusion | flops 17432576 | bytes 2375680 | tf_op jit(solution)/shard_map/chrs,schd->rchd/dot_general | solution.py:58
  103.7 1.5 copy.51
  105.2 6.8 %all-to-all-start.3 = ((bf16[16,64,4,128]{3,2,1,0:T(4,128)(2,1)}), bf16[16,64,4,128]{3,2,1,0:T(4,128)(2,1)S(1)}, u32[]{:S(2)}, u32[]{:S(2)}) async-start(bf16[16,64,4,128]{3,2,1,0:T(4,128)(2,1)} %copy.51), calls=%async_computation.3 | async-start | bytes 2097152 | tf_op jit(solution)/shard_map/all_to_all | solution.py:61
  112.0 0.2 reduce-scatter.2.cloned.1.call-start
  112.2 7.1 %fusion.12 = bf16[4,1024,128]{1,2,0:T(8,128)(2,1)S(1)} fusion(f32[4,1024,1024]{1,2,0:T(8,128)} %get-tuple-element.16, f32[4,1024]{1,0:T(4,128)S(1)} %get-tuple-element.15, bf16[1,1024,1,2,4,128]{1,5,4,3,2,0:T(8,128)(2,1)S(1)} %bitcast.60), kind=kOutput, calls=%fused_computation.21 | convolution fusion | flops 1082654720 | bytes 18890752 | tf_op jit(solution)/shard_map/while/body/eval_jaxpr/hqk,khd->qhd/dot_general | solution.py:39
  119.3 10.3 %fusion.8 = f32[1024,4096]{1,0:T(8,128)} fusion(bf16[1024,512]{0,1:T(8,128)(2,1)S(1)} %bitcast.69, bf16[1,2,512,4096]{3,2,1,0:T(8,128)(2,1)} %bitcast.67), kind=kOutput, calls=%fused_computation.14 | convolution fusion | flops 4294967296 | bytes 22020096 | tf_op jit(solution)/shard_map/dot_general | solution.py:80
  129.6 5.3 %all-to-all-done.3 = bf16[16,64,4,128]{3,2,1,0:T(4,128)(2,1)S(1)} async-done(((bf16[16,64,4,128]{3,2,1,0:T(4,128)(2,1)}), bf16[16,64,4,128]{3,2,1,0:T(4,128)(2,1)S(1)}, u32[]{:S(2)}, u32[]{:S(2)}) %all-to-all-start.3) | async-done | bytes 1048608 | tf_op jit(solution)/shard_map/all_to_all | solution.py:61
  134.9 11.3 %fusion.3 = bf16[1,1024,4096]{2,1,0:T(8,128)(2,1)} fusion(f32[1024,4096]{1,0:T(8,128)} %fusion.8, bf16[1,2,512,4096]{3,2,1,0:T(8,128)(2,1)} %bitcast.68, bf16[128,8,4,128]{3,2,1,0:T(4,128)(2,1)S(1)} %bitcast.66), kind=kOutput, calls=%fused_computation.7 | convolution fusion | flops 4303355904 | bytes 30408704 | tf_op jit(solution)/shard_map/dot_general | solution.py:83
  146.2 0.0 reduce-scatter.2.cloned.1.call-update
  146.2 101.6 %reduce-scatter.2.cloned.1.call-done = bf16[1,512,4096]{2,1,0:T(8,128)(2,1)} async-done(((bf16[1,1024,4096]{2,1,0:T(8,128)(2,1)}), bf16[1,512,4096]{2,1,0:T(8,128)(2,1)}) %reduce-scatter.2.cloned.1.call-update) | async-done | bytes 4194320 | tf_op jit(solution)/shard_map/reduce_scatter | solution.py:87
  (3 shorter events, 0.0 us)
Async XLA Ops:
  9.4 13.1 %copy-start = (bf16[1,1024,1024]{1,2,0:T(8,128)(2,1)}, bf16[1,1024,1024]{1,2,0:T(8,128)(2,1)S(1)}, u32[]{:S(2)}) copy-start(bf16[1,1024,1024]{1,2,0:T(8,128)(2,1)S(1)} %copy.35) | copy-start | bytes 6291460
  11.1 30.3 %all-to-all-start = ((bf16[1,1024,4,128]{3,2,0,1:T(4,128)(2,1)}), bf16[1,1024,4,128]{3,2,0,1:T(4,128)(2,1)S(1)}, u32[]{:S(2)}, u32[]{:S(2)}) async-start(bf16[1,1024,4,128]{3,2,0,1:T(4,128)(2,1)} %copy.41), calls=%async_computation | async-start | bytes 2097152 | tf_op jit(solution)/shard_map/all_to_all | solution.py:72
  41.4 9.7 %copy-start.1 = (bf16[1,1024,4,128]{3,2,0,1:T(4,128)(2,1)}, bf16[1,1024,4,128]{3,2,0,1:T(4,128)(2,1)S(1)}, u32[]{:S(2)}) copy-start(bf16[1,1024,4,128]{3,2,0,1:T(4,128)(2,1)S(1)} %all-to-all-done) | copy-start | bytes 3145732
  41.4 29.8 %all-to-all-start.1 = ((bf16[1,1024,4,128]{3,2,0,1:T(4,128)(2,1)}), bf16[1,1024,4,128]{3,2,0,1:T(4,128)(2,1)}, u32[]{:S(2)}, u32[]{:S(2)}) async-start(bf16[1,1024,4,128]{3,2,0,1:T(4,128)(2,1)} %copy.43), calls=%async_computation.1 | async-start | bytes 2097152 | tf_op jit(solution)/shard_map/all_to_all | solution.py:73
  71.2 29.8 %all-to-all-start.2 = ((bf16[1,1024,4,128]{3,2,0,1:T(4,128)(2,1)}), bf16[1,1024,4,128]{3,2,0,1:T(4,128)(2,1)}, u32[]{:S(2)}, u32[]{:S(2)}) async-start(bf16[1,1024,4,128]{3,2,0,1:T(4,128)(2,1)} %copy.47), calls=%async_computation.2 | async-start | bytes 2097152 | tf_op jit(solution)/shard_map/all_to_all | solution.py:74
  79.4 11.8 %copy-start.2 = (bf16[1,1024,4,128]{3,2,0,1:T(4,128)(2,1)S(1)}, bf16[1,1024,4,128]{3,2,0,1:T(4,128)(2,1)}, u32[]{:S(2)}) copy-start(bf16[1,1024,4,128]{3,2,0,1:T(4,128)(2,1)} %copy-done.1) | copy-start | bytes 3145732
  105.2 29.7 %all-to-all-start.3 = ((bf16[16,64,4,128]{3,2,1,0:T(4,128)(2,1)}), bf16[16,64,4,128]{3,2,1,0:T(4,128)(2,1)S(1)}, u32[]{:S(2)}, u32[]{:S(2)}) async-start(bf16[16,64,4,128]{3,2,1,0:T(4,128)(2,1)} %copy.51), calls=%async_computation.3 | async-start | bytes 2097152 | tf_op jit(solution)/shard_map/all_to_all | solution.py:61
  112.0 135.8 %reduce-scatter.2.cloned.1.call-start = ((), (), s32[]{:S(2)}) async-start(), calls=%async_computation.5 | async-start | bytes 12582912 | tf_op jit(solution)/shard_map/reduce_scatter | solution.py:87
Sparse Core Ops, SparseCore 0:
  146.3 101.4 reduce-scatter.1
where the time goes:
time: 255 us
  waiting for transfers between devices  147 us (58%)
  matrix products  47.8 us (19%)
  starting transfers between devices  28.1 us (11%)
  local copies, waits for them, and re-layouts  17.1 us (7%)
  between operations  13.5 us (5%)
    reduce_scatter x1, waiting for transfers between devices, on_device(): lax.psum_scatter(partial_value.astype(jnp.bfloat16), 'head', scatter_dime...  102 us
    all_to_all x1, waiting for transfers between devices, on_device(): lax.all_to_all(col_triple[1], 'ctx', split_axis=1, concat_axis=0, tiled=T...  18.5 us
    sub x2, matrix products, normalized(): expo = jnp.exp(scores - top)  16.4 us
    all_to_all x1, waiting for transfers between devices, on_device(): lax.all_to_all(col_triple[0], 'ctx', split_axis=1, concat_axis=0, tiled=T...  16.2 us
    dot_general x1, matrix products, on_device(): jnp.dot(col_out.reshape((rows_dev * stride, -1)), col_weights, preferred_...  11.3 us
    dot_general x1, matrix products, on_device(): jnp.dot(row_out.reshape((rows_dev * stride, -1)), row_weights, preferred_...  10.3 us
    unnamed x9, local copies, waits for them, and re-layouts  9.69 us
    all_to_all x1, starting transfers between devices, on_device(): lax.all_to_all(col_triple[0], 'ctx', split_axis=1, concat_axis=0, tiled=T...  7.41 us
  transfers between devices with their start and end apart: 5, of which 5 were waited for; matrix products, arithmetic and copies ran while one was open for 18% of the time, Pallas kernels for 0%

commit v1 on v0

--- a/solution.py
+++ b/solution.py
@@ -70,7 +70,12 @@
     col_out = column_attention(
         (
             lax.all_to_all(col_triple[0], "ctx", split_axis=1, concat_axis=0, tiled=True),
-            lax.all_to_all(col_triple[1], "ctx", split_axis=1, concat_axis=0, tiled=True),
+            jnp.concatenate(
+                lax.all_to_all(
+                    jnp.stack(jnp.split(col_triple[1], lax.axis_size("ctx"), axis=1)), "ctx", 0, 0
+                ),
+                axis=0,
+            ),
             lax.all_to_all(col_triple[2], "ctx", split_axis=1, concat_axis=0, tiled=True),
         )
     )

time: 255 us -> 275 us (1.078)
  local copies, waits for them, and re-layouts: 17.1 us -> 55.2 us
  waiting for transfers between devices: 147 us -> 130 us
    split x0 -> x17, local copies, waits for them, and re-layouts: none -> 23.6 us  [on_device(): jnp.split(col_triple[1], lax.axis_size('ctx'), axis=1)]
    all_to_all x1, waiting for transfers between devices: 16.2 us -> 0.01 us  [on_device(): lax.all_to_all(col_triple[0], 'ctx', split_axis=1, concat_axis=0, tiled=T...]
    unnamed x9 -> x24, local copies, waits for them, and re-layouts: 9.69 us -> 21.9 us
    another operation x6 -> x5, local copies, waits for them, and re-layouts: 5.93 us -> 5.59 us  [split_kinds(): shaped[:, :, :, parity]]
  transfers between devices with their start and end apart: 5 -> 5, of which waited for: 5 -> 4; matrix products, arithmetic and copies ran while one was open for 18% -> 30% of each run, Pallas kernels for 0% -> 0%
where the time goes in v1:
time: 275 us; the launch traced here: 273 us
  waiting for transfers between devices  130 us (47%)
  local copies, waits for them, and re-layouts  55.2 us (20%)
  matrix products  45.7 us (17%)
  starting transfers between devices  27.4 us (10%)
  between operations  13.5 us (5%)
    reduce_scatter x1, waiting for transfers between devices, on_device(): lax.psum_scatter(partial_value.astype(jnp.bfloat16), 'head', scatter_dime...  102 us
    split x17, local copies, waits for them, and re-layouts, on_device(): jnp.split(col_triple[1], lax.axis_size('ctx'), axis=1)  23.6 us
    unnamed x24, local copies, waits for them, and re-layouts  21.9 us
    all_to_all x1, waiting for transfers between devices, on_device(): lax.all_to_all(jnp.stack(jnp.split(col_triple[1], lax.axis_size('ctx'), a...  16.2 us
    sub x2, matrix products, normalized(): expo = jnp.exp(scores - top)  14.9 us
    dot_general x1, matrix products, on_device(): jnp.dot(col_out.reshape((rows_dev * stride, -1)), col_weights, preferred_...  11.3 us
    dot_general x1, matrix products, on_device(): jnp.dot(row_out.reshape((rows_dev * stride, -1)), row_weights, preferred_...  10.3 us
    all_to_all x1, starting transfers between devices, on_device(): lax.all_to_all(col_triple[0], 'ctx', split_axis=1, concat_axis=0, tiled=T...  7.41 us
  transfers between devices with their start and end apart: 5, of which 4 were waited for; matrix products, arithmetic and copies ran while one was open for 30% of the time, Pallas kernels for 0%

profile of v1, /device:TPU:0, one launch (start us, length us, event | category | flops | bytes accessed | tf_op | source)
XLA Modules:
  0.0 272.9 jit_solution(15023224479432862639)
XLA Ops:
  6.5 2.9 %copy.621 = bf16[1,1024,1024]{1,2,0:T(8,128)(2,1)S(1)} copy(bf16[1,1024,1024]{2,1,0:T(8,128)(2,1)} %param.4) | data formatting | bytes 4194304 | tf_op args[0]
  10.9 7.4 %all-to-all-start.1 = ((bf16[1,1024,4,128]{3,2,0,1:T(4,128)(2,1)}), bf16[1,1024,4,128]{3,2,0,1:T(4,128)(2,1)S(1)}, u32[]{:S(2)}, u32[]{:S(2)}) async-start(bf16[1,1024,4,128]{3,2,0,1:T(4,128)(2,1)} %copy.645), calls=%async_computation.1 | async-start | bytes 2097152 | tf_op jit(solution)/shard_map/all_to_all | solution.py:72
  18.3 3.9 %copy.623 = bf16[1,1024,1024]{1,2,0:T(8,128)(2,1)} copy(bf16[1,1024,1024]{2,1,0:T(8,128)(2,1)} %param.5) | data formatting | bytes 4194304 | tf_op args[1]
  23.6 1.6 fusion.30
  25.2 1.6 copy.642
  26.8 1.6 copy.641
  28.4 1.6 copy.640
  30.1 1.6 copy.639
  31.7 1.6 copy.638
  33.3 1.6 copy.637
  34.9 1.6 copy.636
  36.5 1.6 copy.635
  38.2 1.6 copy.634
  39.8 1.6 copy.633
  41.4 1.6 copy.632
  43.0 1.6 copy.631
  44.6 1.6 copy.630
  59.2 1.9 copy.643
  61.1 6.1 %all-to-all-start = ((bf16[16,1,64,4,128]{4,3,2,1,0:T(4,128)(2,1)}), bf16[16,1,64,4,128]{4,3,2,1,0:T(4,128)(2,1)}, u32[]{:S(2)}, u32[]{:S(2)}) async-start(bf16[16,1,64,4,128]{4,3,2,1,0:T(4,128)(2,1)} %copy.643), calls=%async_computation | async-start | bytes 2097152 | tf_op jit(solution)/shard_map/all_to_all | solution.py:74
  67.1 4.0 %copy.625 = bf16[1,1024,1024]{1,2,0:T(8,128)(2,1)} copy(bf16[1,1024,1024]{2,1,0:T(8,128)(2,1)} %param.6) | data formatting | bytes 4194304 | tf_op args[2]
  73.9 16.2 %all-to-all-done = bf16[16,1,64,4,128]{4,3,2,1,0:T(4,128)(2,1)} async-done(((bf16[16,1,64,4,128]{4,3,2,1,0:T(4,128)(2,1)}), bf16[16,1,64,4,128]{4,3,2,1,0:T(4,128)(2,1)}, u32[]{:S(2)}, u32[]{:S(2)}) %all-to-all-start) | async-done | bytes 1048608 | tf_op jit(solution)/shard_map/all_to_all | solution.py:74
  90.1 6.9 %all-to-all-start.2 = ((bf16[1,1024,4,128]{3,2,0,1:T(4,128)(2,1)}), bf16[1,1024,4,128]{3,2,0,1:T(4,128)(2,1)}, u32[]{:S(2)}, u32[]{:S(2)}) async-start(bf16[1,1024,4,128]{3,2,0,1:T(4,128)(2,1)} %copy.648), calls=%async_computation.2 | async-start | bytes 2097152 | tf_op jit(solution)/shard_map/all_to_all | solution.py:79
  98.3 11.6 %fusion.31 = (f32[4,1024]{1,0:T(4,128)S(1)}, f32[4,1024,1024]{1,2,0:T(8,128)}) fusion(pred[1024,1024]{0,1:T(8,128)(4,1)} %iota_compare_fusion, bf16[1,1024,1,2,4,128]{1,5,4,3,2,0:T(8,128)(2,1)S(1)} %bitcast.105, bf16[1,1024,1,2,4,128]{1,5,4,3,2,0:T(8,128)(2,1)} %bitcast.107), kind=kOutput, calls=%fused_computation.64 | convolution fusion | flops 1090520064 | bytes 19939328 | tf_op jit(solution)/shard_map/while/body/eval_jaxpr/sub | solution.py:19
  109.9 3.3 %fusion.32 = (f32[64,4,16]{2,1,0:T(4,128)S(1)}, f32[64,4,16,16]{2,3,1,0:T(8,128)S(1)}) fusion(pred[16,16]{0,1:T(8,128)(4,1)S(1)} %iota_compare_fusion.1, bf16[16,64,4,128]{3,2,1,0:T(4,128)(2,1)S(1)} %bitcast.110, bf16[16,1,64,4,128]{4,3,2,1,0:T(4,128)(2,1)} %all-to-all-done), kind=kOutput, calls=%fused_computation.65 | convolution fusion | flops 17039376 | bytes 2375936 | tf_op jit(solution)/shard_map/sub | solution.py:19
  113.2 6.7 %all-to-all-done.2 = bf16[1,1024,4,128]{3,2,0,1:T(4,128)(2,1)} async-done(((bf16[1,1024,4,128]{3,2,0,1:T(4,128)(2,1)}), bf16[1,1024,4,128]{3,2,0,1:T(4,128)(2,1)}, u32[]{:S(2)}, u32[]{:S(2)}) %all-to-all-start.2) | async-done | bytes 1048608 | tf_op jit(solution)/shard_map/all_to_all | solution.py:79
  119.9 2.1 fusion.13
  123.4 6.8 %all-to-all-start.3 = ((bf16[16,64,4,128]{3,2,1,0:T(4,128)(2,1)}), bf16[16,64,4,128]{3,2,1,0:T(4,128)(2,1)S(1)}, u32[]{:S(2)}, u32[]{:S(2)}) async-start(bf16[16,64,4,128]{3,2,1,0:T(4,128)(2,1)} %copy.652), calls=%async_computation.3 | async-start | bytes 2097152 | tf_op jit(solution)/shard_map/all_to_all | solution.py:61
  130.5 7.1 %fusion.12 = bf16[4,1024,128]{1,2,0:T(8,128)(2,1)S(1)} fusion(f32[4,1024,1024]{1,2,0:T(8,128)} %get-tuple-element.40, f32[4,1024]{1,0:T(4,128)S(1)} %get-tuple-element.39, bf16[1,1024,1,2,4,128]{1,5,4,3,2,0:T(8,128)(2,1)S(1)} %bitcast.109), kind=kOutput, calls=%fused_computation.21 | convolution fusion | flops 1082654720 | bytes 18890752 | tf_op jit(solution)/shard_map/while/body/eval_jaxpr/hqk,khd->qhd/dot_general | solution.py:39
  137.6 10.3 %fusion.8 = f32[1024,4096]{1,0:T(8,128)} fusion(bf16[1024,512]{0,1:T(8,128)(2,1)S(1)} %bitcast.114, bf16[1,2,512,4096]{3,2,1,0:T(8,128)(2,1)} %bitcast.112), kind=kOutput, calls=%fused_computation.14 | convolution fusion | flops 4294967296 | bytes 22020096 | tf_op jit(solution)/shard_map/dot_general | solution.py:85
  147.9 5.2 %all-to-all-done.3 = bf16[16,64,4,128]{3,2,1,0:T(4,128)(2,1)S(1)} async-done(((bf16[16,64,4,128]{3,2,1,0:T(4,128)(2,1)}), bf16[16,64,4,128]{3,2,1,0:T(4,128)(2,1)S(1)}, u32[]{:S(2)}, u32[]{:S(2)}) %all-to-all-start.3) | async-done | bytes 1048608 | tf_op jit(solution)/shard_map/all_to_all | solution.py:61
  153.1 11.3 %fusion.3 = bf16[1,1024,4096]{2,1,0:T(8,128)(2,1)} fusion(f32[1024,4096]{1,0:T(8,128)} %fusion.8, bf16[1,2,512,4096]{3,2,1,0:T(8,128)(2,1)} %bitcast.113, bf16[128,8,4,128]{3,2,1,0:T(4,128)(2,1)S(1)} %bitcast.111), kind=kOutput, calls=%fused_computation.7 | convolution fusion | flops 4303355904 | bytes 30408704 | tf_op jit(solution)/shard_map/dot_general | solution.py:88
  164.4 101.6 %reduce-scatter.2.cloned.1.call-done = bf16[1,512,4096]{2,1,0:T(8,128)(2,1)} async-done(((bf16[1,1024,4096]{2,1,0:T(8,128)(2,1)}), bf16[1,512,4096]{2,1,0:T(8,128)(2,1)}) %reduce-scatter.2.cloned.1.call-update) | async-done | bytes 4194320 | tf_op jit(solution)/shard_map/reduce_scatter | solution.py:92
  (36 shorter events, 21.6 us)
Async XLA Ops:
  10.9 50.2 %all-to-all-start.1 = ((bf16[1,1024,4,128]{3,2,0,1:T(4,128)(2,1)}), bf16[1,1024,4,128]{3,2,0,1:T(4,128)(2,1)S(1)}, u32[]{:S(2)}, u32[]{:S(2)}) async-start(bf16[1,1024,4,128]{3,2,0,1:T(4,128)(2,1)} %copy.645), calls=%async_computation.1 | async-start | bytes 2097152 | tf_op jit(solution)/shard_map/all_to_all | solution.py:72
  61.1 10.0 %copy-start.1 = (bf16[1,1024,4,128]{3,2,0,1:T(4,128)(2,1)}, bf16[1,1024,4,128]{3,2,0,1:T(4,128)(2,1)S(1)}, u32[]{:S(2)}) copy-start(bf16[1,1024,4,128]{3,2,0,1:T(4,128)(2,1)S(1)} %all-to-all-done.1) | copy-start | bytes 3145732
  61.1 29.0 %all-to-all-start = ((bf16[16,1,64,4,128]{4,3,2,1,0:T(4,128)(2,1)}), bf16[16,1,64,4,128]{4,3,2,1,0:T(4,128)(2,1)}, u32[]{:S(2)}, u32[]{:S(2)}) async-start(bf16[16,1,64,4,128]{4,3,2,1,0:T(4,128)(2,1)} %copy.643), calls=%async_computation | async-start | bytes 2097152 | tf_op jit(solution)/shard_map/all_to_all | solution.py:74
  90.1 29.8 %all-to-all-start.2 = ((bf16[1,1024,4,128]{3,2,0,1:T(4,128)(2,1)}), bf16[1,1024,4,128]{3,2,0,1:T(4,128)(2,1)}, u32[]{:S(2)}, u32[]{:S(2)}) async-start(bf16[1,1024,4,128]{3,2,0,1:T(4,128)(2,1)} %copy.648), calls=%async_computation.2 | async-start | bytes 2097152 | tf_op jit(solution)/shard_map/all_to_all | solution.py:79
  98.3 11.6 %copy-start.2 = (bf16[1,1024,4,128]{3,2,0,1:T(4,128)(2,1)S(1)}, bf16[1,1024,4,128]{3,2,0,1:T(4,128)(2,1)}, u32[]{:S(2)}) copy-start(bf16[1,1024,4,128]{3,2,0,1:T(4,128)(2,1)} %copy-done.1) | copy-start | bytes 3145732
  122.0 8.5 %copy-start = (bf16[1,1024,1024]{1,2,0:T(8,128)(2,1)S(1)}, bf16[1,1024,1024]{1,2,0:T(8,128)(2,1)}, u32[]{:S(2)}) copy-start(bf16[1,1024,1024]{1,2,0:T(8,128)(2,1)} %copy.625) | copy-start | bytes 6291460
  123.4 29.7 %all-to-all-start.3 = ((bf16[16,64,4,128]{3,2,1,0:T(4,128)(2,1)}), bf16[16,64,4,128]{3,2,1,0:T(4,128)(2,1)S(1)}, u32[]{:S(2)}, u32[]{:S(2)}) async-start(bf16[16,64,4,128]{3,2,1,0:T(4,128)(2,1)} %copy.652), calls=%async_computation.3 | async-start | bytes 2097152 | tf_op jit(solution)/shard_map/all_to_all | solution.py:61
  130.2 135.8 %reduce-scatter.2.cloned.1.call-start = ((), (), s32[]{:S(2)}) async-start(), calls=%async_computation.5 | async-start | bytes 12582912 | tf_op jit(solution)/shard_map/reduce_scatter | solution.py:92
Sparse Core Ops, SparseCore 0:
  164.6 101.4 reduce-scatter.1
